TPU v7x, 32 devices: a whole 2x2x4 slice. The times are simulated.
32 devices in a mesh: grp: 2 (over y), kvp: 4 (over x, core), tp: 4 (over z).
Axes of the slice: x: 2, y: 2, z: 4, core: 2. Of those that a mesh axis runs over, the one named last changes fastest.
Arguments:
- hidden_in: bfloat16 [16, 7168], P('grp'), parts along dimension 0, may hold values from -3 to 3
- queries_nope: bfloat16 [16, 128, 128], P('grp', ('kvp', 'tp')), parts along dimension 0, may hold values from -6 to 6
- queries_rope: bfloat16 [16, 128, 64], P('grp', ('kvp', 'tp')), parts along dimension 0, may hold values from -26 to 26
- cache: bfloat16 [16, 1536, 576], P('grp', 'kvp'), parts along dimension 0, may hold values from -20 to 20
- lengths: int32 [16], P('grp'), parts along dimension 0, may hold values from 128 to 1536, as said below
- w_uk: bfloat16 [128, 128, 512], P(('kvp', 'tp')), may hold values from -0.5 to 0.5
- w_uv: bfloat16 [128, 512, 128], P(('kvp', 'tp')), may hold values from -0.25 to 0.25
- w_out: bfloat16 [16384, 7168], P(('kvp', 'tp')), may hold values from -0.0625 to 0.0625
- norm_gain: float32 [7168], replicated, may hold values from 0.25 to 1.75
- w_gate: bfloat16 [7168, 18432], P(None, ('kvp', 'tp')), may hold values from -0.0625 to 0.0625
- w_up: bfloat16 [7168, 18432], P(None, ('kvp', 'tp')), may hold values from -0.0625 to 0.0625
- w_down: bfloat16 [18432, 7168], P(('kvp', 'tp')), may hold values from -0.0625 to 0.0625
Outputs:
- layer_out: bfloat16 [16, 7168], P('grp', ('kvp', 'tp')), parts along dimension 0
There are 2 independent parts, one for each index of `grp`. A program takes and returns all parts, laid end to end along the dimension named above; an argument that names none is the same for every part. Nothing has to cross between parts.
Inputs may be any that keep to these rules, and one draw needn't show every extreme that they name: `lengths`: every length is a multiple of 128; in every draw some request has the full 1536.
All inputs are finite; a program needn't handle non-finite values.
Results may differ from a plain program's by a relative error of at most 0.04.
Values may be sent and summed in bfloat16 or wider, within the bound.
A program may use at most 128 MiB of HBM per device.

v0:
```python
import jax
import jax.numpy as jnp
from jax import lax
from jax.sharding import PartitionSpec as P


def project(o_lat, w_uv, w_out):
    head_out = jnp.einsum("bhl,hle->bhe", o_lat, w_uv, preferred_element_type=jnp.float32).astype(
        jnp.bfloat16
    )
    return jnp.dot(
        head_out.reshape(head_out.shape[0], -1), w_out, preferred_element_type=jnp.float32
    )


def per_device(
    hidden_in,
    queries_nope,
    queries_rope,
    cache,
    lengths,
    w_uk,
    w_uv,
    w_out,
    norm_gain,
    w_gate,
    w_up,
    w_down,
):
    batch, heads_dev, head_dim = queries_nope.shape
    latent = w_uk.shape[2]
    ctx_dev = cache.shape[1]
    groups = lax.axis_size("kvp")
    score_scale = float(head_dim + queries_rope.shape[2]) ** (-0.5)
    q_lat = jnp.einsum(
        "bhd,hdl->bhl", queries_nope, w_uk, preferred_element_type=jnp.float32
    ).astype(jnp.bfloat16)
    q_lat_all, rope_all = (
        lax.all_gather(q_lat, "kvp", axis=1, tiled=True),
        lax.all_gather(queries_rope, "kvp", axis=1, tiled=True),
    )
    q_full = jnp.concatenate([q_lat_all, rope_all], axis=2)
    scores = (
        jnp.einsum("bhc,btc->bht", q_full, cache, preferred_element_type=jnp.float32) * score_scale
    )
    offset = lax.axis_index("kvp") * ctx_dev
    visible = ((offset + jnp.arange(ctx_dev, dtype=jnp.int32))[None, :] < lengths[:, None])[
        :, None, :
    ]
    masked = jnp.where(visible, scores, jnp.float32(-1e30))
    block_max = jnp.max(masked, axis=2)
    exponent = jnp.where(visible, jnp.exp(masked - block_max[..., None]), jnp.float32(0.0))
    guarded = jnp.maximum(jnp.sum(exponent, axis=2), 1.0)
    log_total = block_max + jnp.log(guarded)
    weights = (exponent / guarded[..., None]).astype(jnp.bfloat16)
    partial_value = jnp.einsum("bht,btc->bhc", weights, cache, preferred_element_type=jnp.float32)[
        ..., :latent
    ]
    blocks = partial_value.reshape(batch, groups, heads_dev, latent)
    block_logs = log_total.reshape(batch, groups, heads_dev)
    part_blocks = lax.all_to_all(
        blocks.astype(jnp.bfloat16), "kvp", split_axis=1, concat_axis=1, tiled=True
    ).astype(blocks.dtype)
    part_logs = lax.all_to_all(
        block_logs.astype(jnp.bfloat16), "kvp", split_axis=1, concat_axis=1, tiled=True
    ).astype(block_logs.dtype)
    highest = jnp.max(part_logs, axis=1)
    overall = highest + jnp.log(jnp.sum(jnp.exp(part_logs - highest[:, None, :]), axis=1))
    scaled = jnp.exp(part_logs - overall[:, None, :])[..., None] * part_blocks
    o_lat = jnp.sum(scaled, axis=1).astype(jnp.bfloat16)
    attention = project(o_lat, w_uv, w_out)
    model_width = norm_gain.shape[0]
    share_width = model_width // lax.axis_size(("kvp", "tp"))
    share_start = lax.axis_index(("kvp", "tp")) * share_width
    attn_whole = lax.psum(attention, ("kvp", "tp"))
    residual = hidden_in.astype(jnp.float32) + attn_whole
    mean_square = jnp.mean(residual * residual, axis=1)
    normed = (residual * lax.rsqrt(mean_square + 1e-06)[:, None] * norm_gain[None, :]).astype(
        jnp.bfloat16
    )
    residual_share = lax.dynamic_slice_in_dim(residual, share_start, share_width, 1)
    gate_proj = jnp.dot(normed, w_gate, preferred_element_type=jnp.float32)
    up_proj = jnp.dot(normed, w_up, preferred_element_type=jnp.float32)
    act = (jax.nn.silu(gate_proj) * up_proj).astype(jnp.bfloat16)
    ffn_terms = jnp.dot(act, w_down, preferred_element_type=jnp.float32)
    ffn_share = lax.psum_scatter(ffn_terms, ("kvp", "tp"), scatter_dimension=1, tiled=True)
    return (residual_share + ffn_share).astype(jnp.bfloat16)


def solution(mesh):
    placed = (
        P("grp", None),
        P("grp", ("kvp", "tp"), None),
        P("grp", ("kvp", "tp"), None),
        P("grp", "kvp", None),
        P("grp"),
        P(("kvp", "tp"), None, None),
        P(("kvp", "tp"), None, None),
        P(("kvp", "tp"), None),
        P(),
        P(None, ("kvp", "tp")),
        P(None, ("kvp", "tp")),
        P(("kvp", "tp"), None),
    )
    return jax.shard_map(
        per_device, mesh=mesh, in_specs=placed, out_specs=P("grp", ("kvp", "tp")), check_vma=False
    )
```

profile of v0, /device:TPU:0, one launch (start us, length us, event | category | flops | bytes accessed | tf_op | source)
XLA Modules:
  0.0 248.7 jit_solution(1045707272200250479)
XLA Ops:
  6.5 0.0 copy-start
  6.5 0.9 copy.24
  7.4 6.3 %all_gather.7 = bf16[8,32,64]{2,0,1:T(8,128)(2,1)S(1)} all-gather(bf16[8,8,64]{2,0,1:T(8,128)(2,1)S(1)} %copy.24), channel_id=1, replica_groups=mesh['grp'=2,'kvp'=4,'tp'=4] {'kvp'}, dimensions={1}, use_global_device_ids=true | all-gather | bytes 40960 | tf_op jit(solution)/shard_map/all_gather | solution.py:40
  13.7 1.5 fusion.2
  15.2 6.3 %all_gather.6 = bf16[8,32,512]{2,0,1:T(8,128)(2,1)S(1)} all-gather(bf16[8,8,512]{2,0,1:T(8,128)(2,1)S(1)} %fusion.2), channel_id=1, replica_groups=mesh['grp'=2,'kvp'=4,'tp'=4] {'kvp'}, dimensions={1}, use_global_device_ids=true | all-gather | bytes 327680 | tf_op jit(solution)/shard_map/all_gather | solution.py:39
  21.5 0.1 copy.25
  21.6 0.7 broadcast_compare_fusion
  22.3 0.0 copy-done
  22.3 0.7 fusion.31
  23.0 0.0 copy-start.3
  23.0 0.7 copy-done.3
  23.8 0.2 fusion.8
  24.0 0.6 add_convert_fusion.1
  24.6 0.8 convert_element_type.50
  25.3 0.6 copy.27
  25.9 3.2 %all-to-all-start = ((bf16[8,4,8]{2,0,1:T(8,128)(2,1)}), bf16[8,4,8]{2,0,1:T(8,128)(2,1)S(1)}, u32[]{:S(2)}, u32[]{:S(2)}) async-start(bf16[8,4,8]{2,0,1:T(8,128)(2,1)} %copy.27), calls=%async_computation | async-start | bytes 16384 | tf_op jit(solution)/shard_map/all_to_all | solution.py:64
  29.2 2.2 fusion.10
  31.4 0.0 copy-start.5
  31.5 0.0 copy-start.4
  31.5 0.7 copy.28
  32.2 0.8 all-to-all-done
  33.0 3.4 %all-to-all-start.1 = ((bf16[8,4,8,512]{3,2,0,1:T(8,128)(2,1)}), bf16[8,4,8,512]{3,2,0,1:T(8,128)(2,1)S(1)}, u32[]{:S(2)}, u32[]{:S(2)}) async-start(bf16[8,4,8,512]{3,2,0,1:T(8,128)(2,1)} %copy.28), calls=%async_computation.1 | async-start | bytes 524288 | tf_op jit(solution)/shard_map/all_to_all | solution.py:61
  36.4 0.0 all-reduce.2.cloned.1.call-start
  36.5 5.8 %all-to-all-done.1 = bf16[8,4,8,512]{3,2,0,1:T(8,128)(2,1)S(1)} async-done(((bf16[8,4,8,512]{3,2,0,1:T(8,128)(2,1)}), bf16[8,4,8,512]{3,2,0,1:T(8,128)(2,1)S(1)}, u32[]{:S(2)}, u32[]{:S(2)}) %all-to-all-start.1) | async-done | bytes 262176 | tf_op jit(solution)/shard_map/all_to_all | solution.py:61
  42.4 0.1 multiply_reduce_fusion
  42.5 8.4 %fusion.4 = f32[8,7168]{1,0:T(8,128)} fusion(bf16[1024,7168]{1,0:T(8,128)(2,1)} %param.19, bf16[8,512,128]{2,1,0:T(8,128)(2,1)} %param.18, bf16[8,8,512]{2,1,0:T(8,128)(2,1)S(1)} %multiply_reduce_fusion), kind=kOutput, calls=%fused_computation.9 | convolution fusion | flops 125837312 | bytes 16023552 | tf_op jit(solution)/shard_map/dot_general | solution.py:11
  50.8 0.0 all-reduce.2.cloned.1.call-update
  50.9 0.0 reduce-scatter.4.cloned.1.call-start
  50.9 89.8 %all-reduce.2.cloned.1.call-done = f32[8,7168]{1,0:T(8,128)} async-done(((f32[8,7168]{1,0:T(8,128)}), f32[8,7168]{1,0:T(8,128)}) %all-reduce.2.cloned.1.call-update) | async-done | bytes 229392 | tf_op jit(solution)/shard_map/psum | solution.py:75
  140.7 0.0 copy-done.5
  140.7 1.1 multiply_reduce_fusion.1
  141.8 0.0 copy-start.2
  141.8 0.7 copy-done.2
  142.5 0.0 copy-done.4
  142.5 8.6 %fusion.30 = f32[8,1152]{1,0:T(8,128)} fusion(bf16[7168,1152]{1,0:T(8,128)(2,1)} %param.21, f32[8,7168]{1,0:T(8,128)S(1)} %get-tuple-element.6, f32[7168]{0:T(1024)S(1)} %copy-done.4, f32[8]{0:T(128)S(1)} %add_rsqrt_fusion), kind=kOutput, calls=%fused_computation.50 | convolution fusion | flops 132292608 | bytes 16810016 | tf_op jit(solution)/shard_map/dot_general | solution.py:82
  151.1 0.0 copy-start.1
  151.1 18.6 %convolution_bitcast_fusion = f32[7168,8]{1,0:T(8,128)} fusion(bf16[1152,7168]{1,0:T(8,128)(2,1)} %param.23, bf16[7168,1152]{1,0:T(8,128)(2,1)} %param.22, f32[8,1152]{1,0:T(8,128)} %fusion.30, f32[8,7168]{1,0:T(8,128)} %copy-done.2, f32[7168]{0:T(1024)} %param.20, f32[8]{0:T(128)S(1)} %add_rsqrt_fusion), kind=kOutput, calls=%fused_computation | convolution fusion | flops 264468480 | bytes 33554464
  169.7 0.0 reduce-scatter.4.cloned.1.call-update
  169.7 69.7 %reduce-scatter.4.cloned.1.call-done = f32[448,8]{1,0:T(8,128)} async-done(((f32[7168,8]{1,0:T(8,128)}), f32[448,8]{1,0:T(8,128)}) %reduce-scatter.4.cloned.1.call-update) | async-done | bytes 14352
  239.4 1.0 copy.32
  240.4 1.4 add_convert_fusion
  241.9 0.0 copy-done.1
  (9 shorter events, 0.1 us)
Async XLA Ops:
  6.5 15.7 %copy-start = (bf16[8,384,576]{1,2,0:T(8,128)(2,1)S(1)}, bf16[8,384,576]{1,2,0:T(8,128)(2,1)}, u32[]{:S(2)}) copy-start(bf16[8,384,576]{1,2,0:T(8,128)(2,1)} %param.15) | copy-start | bytes 10616836
  23.0 0.7 copy-start.3
  25.9 7.0 %all-to-all-start = ((bf16[8,4,8]{2,0,1:T(8,128)(2,1)}), bf16[8,4,8]{2,0,1:T(8,128)(2,1)S(1)}, u32[]{:S(2)}, u32[]{:S(2)}) async-start(bf16[8,4,8]{2,0,1:T(8,128)(2,1)} %copy.27), calls=%async_computation | async-start | bytes 16384 | tf_op jit(solution)/shard_map/all_to_all | solution.py:64
  31.4 109.2 %copy-start.5 = (bf16[8,7168]{1,0:T(8,128)(2,1)S(1)}, bf16[8,7168]{1,0:T(8,128)(2,1)}, u32[]{:S(2)}) copy-start(bf16[8,7168]{1,0:T(8,128)(2,1)} %param.12) | copy-start | bytes 344068
  31.5 111.0 %copy-start.4 = (f32[7168]{0:T(1024)S(1)}, f32[7168]{0:T(1024)}, u32[]{:S(2)}) copy-start(f32[7168]{0:T(1024)} %param.20) | copy-start | bytes 86020
  33.0 9.4 %all-to-all-start.1 = ((bf16[8,4,8,512]{3,2,0,1:T(8,128)(2,1)}), bf16[8,4,8,512]{3,2,0,1:T(8,128)(2,1)S(1)}, u32[]{:S(2)}, u32[]{:S(2)}) async-start(bf16[8,4,8,512]{3,2,0,1:T(8,128)(2,1)} %copy.28), calls=%async_computation.1 | async-start | bytes 524288 | tf_op jit(solution)/shard_map/all_to_all | solution.py:61
  36.4 104.3 %all-reduce.2.cloned.1.call-start = ((), (), s32[]{:S(2)}) async-start(), calls=%async_computation.3 | async-start | bytes 458752 | tf_op jit(solution)/shard_map/psum | solution.py:75
  50.9 188.6 %reduce-scatter.4.cloned.1.call-start = ((), (), s32[]{:S(2)}) async-start(), calls=%async_computation.4 | async-start | bytes 3899392
  141.8 0.7 copy-start.2
  151.1 90.8 %copy-start.1 = (bf16[8,384,576]{1,2,0:T(8,128)(2,1)S(1)}, bf16[8,384,576]{1,2,0:T(8,128)(2,1)}, u32[]{:S(2)}) copy-start(bf16[8,384,576]{1,2,0:T(8,128)(2,1)} %param.15) | copy-start | bytes 10616836
Sparse Core Ops, SparseCore 0:
  51.0 89.6 all-reduce.1
  169.9 69.5 reduce-scatter.3
where the time goes:
time: 249 us
  waiting for transfers between devices  166 us (67%)
  matrix products  40 us (16%)
  between operations  13.5 us (5%)
  blocking collectives  12.6 us (5%)
  starting transfers between devices  6.74 us (3%)
  local copies, waits for them, and re-layouts  5.54 us (2%)
  other arithmetic  4.23 us (2%)
    psum x1, waiting for transfers between devices, per_device(): attn_whole = lax.psum(attention, ('kvp', 'tp'))  89.8 us
    unnamed x3, waiting for transfers between devices  69.7 us
    unnamed x1, matrix products  18.6 us
    dot_general x1, matrix products, per_device(): gate_proj = jnp.dot(normed, w_gate, preferred_element_type=jnp.float32)  8.58 us
    dot_general x1, matrix products, project(): jnp.dot(head_out.reshape(head_out.shape[0], -1), w_out, preferred_element...  8.36 us
    all_gather x1, blocking collectives, per_device(): lax.all_gather(queries_rope, 'kvp', axis=1, tiled=True)  6.3 us
    all_gather x1, blocking collectives, per_device(): lax.all_gather(q_lat, 'kvp', axis=1, tiled=True)  6.27 us
    all_to_all x1, waiting for transfers between devices, per_device(): lax.all_to_all(blocks.astype(jnp.bfloat16), 'kvp', split_axis=1, concat_a...  5.84 us
  transfers between devices with their start and end apart: 4, of which 4 were waited for; matrix products, arithmetic and copies ran while one was open for 1% of the time, Pallas kernels for 0%

commit v1 on v0

--- a/solution.py
+++ b/solution.py
@@ -72,7 +72,9 @@
     model_width = norm_gain.shape[0]
     share_width = model_width // lax.axis_size(("kvp", "tp"))
     share_start = lax.axis_index(("kvp", "tp")) * share_width
-    attn_whole = lax.psum(attention, ("kvp", "tp"))
+    attn_whole = attention
+    for over in ("tp", "kvp"):
+        attn_whole = lax.psum(attn_whole, over)
     residual = hidden_in.astype(jnp.float32) + attn_whole
     mean_square = jnp.mean(residual * residual, axis=1)
     normed = (residual * lax.rsqrt(mean_square + 1e-06)[:, None] * norm_gain[None, :]).astype(

time: 249 us -> 228 us (0.916)
  waiting for transfers between devices: 166 us -> 145 us
    psum x1 -> x2, waiting for transfers between devices: 89.8 us -> 69.9 us  [per_device(): attn_whole = lax.psum(attn_whole, over)]
    unnamed x3 -> x4, waiting for transfers between devices: 69.7 us -> 68.8 us
  transfers between devices with their start and end apart: 4 -> 5, of which waited for: 4 -> 5; matrix products, arithmetic and copies ran while one was open for 1% -> 1% of each run, Pallas kernels for 0% -> 0%
where the time goes in v1:
time: 228 us
  waiting for transfers between devices  145 us (64%)
  matrix products  40 us (18%)
  between operations  13.2 us (6%)
  blocking collectives  12.6 us (6%)
  starting transfers between devices  6.78 us (3%)
  local copies, waits for them, and re-layouts  5.54 us (2%)
  other arithmetic  4.23 us (2%)
    psum x2, waiting for transfers between devices, per_device(): attn_whole = lax.psum(attn_whole, over)  69.9 us
    unnamed x4, waiting for transfers between devices  68.8 us
    unnamed x1, matrix products  18.6 us
    dot_general x1, matrix products, per_device(): gate_proj = jnp.dot(normed, w_gate, preferred_element_type=jnp.float32)  8.58 us
    dot_general x1, matrix products, project(): jnp.dot(head_out.reshape(head_out.shape[0], -1), w_out, preferred_element...  8.36 us
    all_gather x1, blocking collectives, per_device(): lax.all_gather(queries_rope, 'kvp', axis=1, tiled=True)  6.3 us
    all_gather x1, blocking collectives, per_device(): lax.all_gather(q_lat, 'kvp', axis=1, tiled=True)  6.27 us
    all_to_all x1, waiting for transfers between devices, per_device(): lax.all_to_all(blocks.astype(jnp.bfloat16), 'kvp', split_axis=1, concat_a...  5.84 us
  transfers between devices with their start and end apart: 5, of which 5 were waited for; matrix products, arithmetic and copies ran while one was open for 1% of the time, Pallas kernels for 0%

profile of v1, /device:TPU:0, one launch (start us, length us, event | category | flops | bytes accessed | tf_op | source)
XLA Modules:
  0.0 227.6 jit_solution(4861955756876073280)
XLA Ops:
  6.5 0.0 copy-start
  6.5 0.9 copy.24
  7.4 6.3 %all_gather.7 = bf16[8,32,64]{2,0,1:T(8,128)(2,1)S(1)} all-gather(bf16[8,8,64]{2,0,1:T(8,128)(2,1)S(1)} %copy.24), channel_id=1, replica_groups=mesh['grp'=2,'kvp'=4,'tp'=4] {'kvp'}, dimensions={1}, use_global_device_ids=true | all-gather | bytes 40960 | tf_op jit(solution)/shard_map/all_gather | solution.py:40
  13.7 1.5 fusion.2
  15.2 6.3 %all_gather.6 = bf16[8,32,512]{2,0,1:T(8,128)(2,1)S(1)} all-gather(bf16[8,8,512]{2,0,1:T(8,128)(2,1)S(1)} %fusion.2), channel_id=1, replica_groups=mesh['grp'=2,'kvp'=4,'tp'=4] {'kvp'}, dimensions={1}, use_global_device_ids=true | all-gather | bytes 327680 | tf_op jit(solution)/shard_map/all_gather | solution.py:39
  21.5 0.1 copy.25
  21.6 0.7 broadcast_compare_fusion
  22.3 0.0 copy-done
  22.3 0.7 fusion.31
  23.0 0.0 copy-start.3
  23.0 0.7 copy-done.3
  23.8 0.2 fusion.8
  24.0 0.6 add_convert_fusion.1
  24.6 0.8 convert_element_type.50
  25.3 0.6 copy.27
  25.9 3.2 %all-to-all-start = ((bf16[8,4,8]{2,0,1:T(8,128)(2,1)}), bf16[8,4,8]{2,0,1:T(8,128)(2,1)S(1)}, u32[]{:S(2)}, u32[]{:S(2)}) async-start(bf16[8,4,8]{2,0,1:T(8,128)(2,1)} %copy.27), calls=%async_computation | async-start | bytes 16384 | tf_op jit(solution)/shard_map/all_to_all | solution.py:64
  29.2 2.2 fusion.10
  31.4 0.0 copy-start.5
  31.5 0.0 copy-start.4
  31.5 0.7 copy.28
  32.2 0.8 all-to-all-done
  33.0 3.4 %all-to-all-start.1 = ((bf16[8,4,8,512]{3,2,0,1:T(8,128)(2,1)}), bf16[8,4,8,512]{3,2,0,1:T(8,128)(2,1)S(1)}, u32[]{:S(2)}, u32[]{:S(2)}) async-start(bf16[8,4,8,512]{3,2,0,1:T(8,128)(2,1)} %copy.28), calls=%async_computation.1 | async-start | bytes 524288 | tf_op jit(solution)/shard_map/all_to_all | solution.py:61
  36.4 0.0 all-reduce.3.cloned.1.call-start
  36.5 5.8 %all-to-all-done.1 = bf16[8,4,8,512]{3,2,0,1:T(8,128)(2,1)S(1)} async-done(((bf16[8,4,8,512]{3,2,0,1:T(8,128)(2,1)}), bf16[8,4,8,512]{3,2,0,1:T(8,128)(2,1)S(1)}, u32[]{:S(2)}, u32[]{:S(2)}) %all-to-all-start.1) | async-done | bytes 262176 | tf_op jit(solution)/shard_map/all_to_all | solution.py:61
  42.4 0.1 multiply_reduce_fusion
  42.5 8.4 %fusion.4 = f32[8,7168]{1,0:T(8,128)} fusion(bf16[1024,7168]{1,0:T(8,128)(2,1)} %param.19, bf16[8,512,128]{2,1,0:T(8,128)(2,1)} %param.18, bf16[8,8,512]{2,1,0:T(8,128)(2,1)S(1)} %multiply_reduce_fusion), kind=kOutput, calls=%fused_computation.9 | convolution fusion | flops 125837312 | bytes 16023552 | tf_op jit(solution)/shard_map/dot_general | solution.py:11
  50.8 0.0 all-reduce.3.cloned.1.call-update
  50.9 0.0 all-reduce.5.cloned.1.call-start
  50.9 35.7 %all-reduce.3.cloned.1.call-done = f32[8,7168]{1,0:T(8,128)} async-done(((f32[8,7168]{1,0:T(8,128)}), f32[8,7168]{1,0:T(8,128)}) %all-reduce.3.cloned.1.call-update) | async-done | bytes 229392 | tf_op jit(solution)/shard_map/psum | solution.py:77
  86.6 0.0 all-reduce.5.cloned.1.call-update
  86.6 0.0 reduce-scatter.4.cloned.1.call-start
  86.6 34.2 %all-reduce.5.cloned.1.call-done = f32[8,7168]{1,0:T(8,128)} async-done(((f32[8,7168]{1,0:T(8,128)}), f32[8,7168]{1,0:T(8,128)}) %all-reduce.5.cloned.1.call-update) | async-done | bytes 229392 | tf_op jit(solution)/shard_map/psum | solution.py:77
  120.9 0.0 copy-done.5
  120.9 1.1 multiply_reduce_fusion.1
  122.0 0.0 copy-start.2
  122.0 0.7 copy-done.2
  122.7 0.0 copy-done.4
  122.7 8.6 %fusion.30 = f32[8,1152]{1,0:T(8,128)} fusion(bf16[7168,1152]{1,0:T(8,128)(2,1)} %param.21, f32[8,7168]{1,0:T(8,128)S(1)} %get-tuple-element.6, f32[7168]{0:T(1024)S(1)} %copy-done.4, f32[8]{0:T(128)S(1)} %add_rsqrt_fusion), kind=kOutput, calls=%fused_computation.50 | convolution fusion | flops 132292608 | bytes 16810016 | tf_op jit(solution)/shard_map/dot_general | solution.py:84
  131.2 0.0 copy-start.1
  131.2 18.6 %convolution_bitcast_fusion = f32[7168,8]{1,0:T(8,128)} fusion(bf16[1152,7168]{1,0:T(8,128)(2,1)} %param.23, bf16[7168,1152]{1,0:T(8,128)(2,1)} %param.22, f32[8,1152]{1,0:T(8,128)} %fusion.30, f32[8,7168]{1,0:T(8,128)} %copy-done.2, f32[7168]{0:T(1024)} %param.20, f32[8]{0:T(128)S(1)} %add_rsqrt_fusion), kind=kOutput, calls=%fused_computation | convolution fusion | flops 264468480 | bytes 33554464
  149.9 0.0 reduce-scatter.4.cloned.1.call-update
  149.9 68.7 %reduce-scatter.4.cloned.1.call-done = f32[448,8]{1,0:T(8,128)} async-done(((f32[7168,8]{1,0:T(8,128)}), f32[448,8]{1,0:T(8,128)}) %reduce-scatter.4.cloned.1.call-update) | async-done | bytes 14352
  218.6 1.0 copy.32
  219.7 1.4 add_convert_fusion
  221.1 0.0 copy-done.1
  (9 shorter events, 0.1 us)
Async XLA Ops:
  6.5 15.7 %copy-start = (bf16[8,384,576]{1,2,0:T(8,128)(2,1)S(1)}, bf16[8,384,576]{1,2,0:T(8,128)(2,1)}, u32[]{:S(2)}) copy-start(bf16[8,384,576]{1,2,0:T(8,128)(2,1)} %param.15) | copy-start | bytes 10616836
  23.0 0.7 copy-start.3
  25.9 7.0 %all-to-all-start = ((bf16[8,4,8]{2,0,1:T(8,128)(2,1)}), bf16[8,4,8]{2,0,1:T(8,128)(2,1)S(1)}, u32[]{:S(2)}, u32[]{:S(2)}) async-start(bf16[8,4,8]{2,0,1:T(8,128)(2,1)} %copy.27), calls=%async_computation | async-start | bytes 16384 | tf_op jit(solution)/shard_map/all_to_all | solution.py:64
  31.4 89.4 %copy-start.5 = (bf16[8,7168]{1,0:T(8,128)(2,1)S(1)}, bf16[8,7168]{1,0:T(8,128)(2,1)}, u32[]{:S(2)}) copy-start(bf16[8,7168]{1,0:T(8,128)(2,1)} %param.12) | copy-start | bytes 344068
  31.5 91.2 %copy-start.4 = (f32[7168]{0:T(1024)S(1)}, f32[7168]{0:T(1024)}, u32[]{:S(2)}) copy-start(f32[7168]{0:T(1024)} %param.20) | copy-start | bytes 86020
  33.0 9.4 %all-to-all-start.1 = ((bf16[8,4,8,512]{3,2,0,1:T(8,128)(2,1)}), bf16[8,4,8,512]{3,2,0,1:T(8,128)(2,1)S(1)}, u32[]{:S(2)}, u32[]{:S(2)}) async-start(bf16[8,4,8,512]{3,2,0,1:T(8,128)(2,1)} %copy.28), calls=%async_computation.1 | async-start | bytes 524288 | tf_op jit(solution)/shard_map/all_to_all | solution.py:61
  36.4 50.2 %all-reduce.3.cloned.1.call-start = ((), (), s32[]{:S(2)}) async-start(), calls=%async_computation.3 | async-start | bytes 458752 | tf_op jit(solution)/shard_map/psum | solution.py:77
  50.9 70.0 %all-reduce.5.cloned.1.call-start = ((), (), s32[]{:S(2)}) async-start(), calls=%async_computation.4 | async-start | bytes 458752 | tf_op jit(solution)/shard_map/psum | solution.py:77
  86.6 132.0 %reduce-scatter.4.cloned.1.call-start = ((), (), s32[]{:S(2)}) async-start(), calls=%async_computation.5 | async-start | bytes 3899392
  122.0 0.7 copy-start.2
  131.2 89.8 %copy-start.1 = (bf16[8,384,576]{1,2,0:T(8,128)(2,1)S(1)}, bf16[8,384,576]{1,2,0:T(8,128)(2,1)}, u32[]{:S(2)}) copy-start(bf16[8,384,576]{1,2,0:T(8,128)(2,1)} %param.15) | copy-start | bytes 10616836
Sparse Core Ops, SparseCore 0:
  51.0 35.5 all-reduce.2
  88.9 31.9 all-reduce.4
  150.0 68.5 reduce-scatter.3
